TPU v7x, 32 devices: a whole 2x2x4 slice. The times are simulated.
32 devices in a mesh: row: 4 (over y, core), col: 8 (over z, x).
Axes of the slice: x: 2, y: 2, z: 4, core: 2. Of those that a mesh axis runs over, the one named last changes fastest.
Arguments:
- first_acts: bfloat16 [2048, 18944], P('col', 'row'), may hold values from -320 to 320, as said below
- second_acts: bfloat16 [2048, 18944], P('row', 'col'), may hold values from -320 to 320, as said below
Outputs:
- row_potential: float32 [18944], P('row')
- column_potential: float32 [18944], P('col')
Inputs may be any that keep to these rules, and one draw needn't show every extreme that they name: `first_acts`: real-valued activations. `second_acts`: real-valued activations.
All inputs are finite; a program needn't handle non-finite values.
Results may differ from a plain program's by a relative error of at most 0.0003.
Values may be sent and summed in bfloat16 or wider, within the bound.
A program may use at most 128 MiB of HBM per device.

v0:
```python
import math

import jax
import jax.numpy as jnp
from jax import lax
from jax.sharding import PartitionSpec as P

NEUR = 18944
SAMP = 2048
ITERS = 4


entropy_scale = 0.004


def row_lse(scores, log_share):
    highest = jnp.max(scores, 1)
    totals = jnp.sum(jnp.exp(scores - highest[:, None]), 1)
    members = lax.axis_size("col")
    maxima, sums = (
        lax.all_to_all(
            highest.reshape(members, -1), "col", split_axis=0, concat_axis=0, tiled=True
        ),
        lax.all_to_all(totals.reshape(members, -1), "col", split_axis=0, concat_axis=0, tiled=True),
    )
    overall = jnp.max(maxima, 0)
    merged_sum = jnp.sum(sums * jnp.exp(maxima - overall[None, :]), 0)
    own_part = log_share - (overall + jnp.log(merged_sum))
    return lax.all_gather(own_part, "col", axis=0, tiled=True)


def col_lse(scores, log_share):
    highest = jnp.max(scores, 0)
    totals = jnp.sum(jnp.exp(scores - highest[None, :]), 0)
    members = lax.axis_size("row")
    maxima, sums = (
        lax.all_to_all(
            highest.reshape(members, -1), "row", split_axis=0, concat_axis=0, tiled=True
        ),
        lax.all_to_all(totals.reshape(members, -1), "row", split_axis=0, concat_axis=0, tiled=True),
    )
    overall = jnp.max(maxima, 0)
    merged_sum = jnp.sum(sums * jnp.exp(maxima - overall[None, :]), 0)
    own_part = log_share - (overall + jnp.log(merged_sum))
    return lax.all_gather(own_part, "row", axis=0, tiled=True)


def shards(first_acts, second_acts):
    full_second = lax.all_gather(second_acts, "row", axis=0, tiled=True)
    rows_here = first_acts.shape[1]
    cols_here = second_acts.shape[1]
    segment = lax.all_gather(first_acts, "col", axis=0, tiled=True)
    products = lax.dot_general(
        segment, full_second, (((0,), (0,)), ((), ())), preferred_element_type=jnp.float32
    )
    widened = segment.astype(jnp.float32)
    products, first_squares = (products, jnp.sum(widened * widened, 0))
    second_wide = full_second.astype(jnp.float32)
    second_squares = jnp.sum(second_wide * second_wide, 0)
    inv_first = 1.0 / jnp.sqrt(first_squares / SAMP + 1e-06)
    inv_second = 1.0 / jnp.sqrt(second_squares / SAMP + 1e-06)
    logk = products * inv_first[:, None] * inv_second[None, :] * (1.0 / (SAMP * entropy_scale))
    log_share = -math.log(NEUR)
    row_potential = jnp.zeros((rows_here,), jnp.float32)
    column_potential = jnp.zeros((cols_here,), jnp.float32)
    for step in range(ITERS):
        row_potential = row_lse(column_potential[None, :] + logk, log_share)
        column_potential = col_lse(row_potential[:, None] + logk, log_share)
    return (row_potential, column_potential)


def solution(mesh):
    return jax.shard_map(
        shards,
        mesh=mesh,
        in_specs=(P("col", "row"), P("row", "col")),
        out_specs=(P("row"), P("col")),
        check_vma=False,
    )
```

profile of v0, /device:TPU:0, one launch (start us, length us, event | category | flops | bytes accessed | tf_op | source)
XLA Modules:
  0.0 1064.9 jit_solution(205873519118053908)
XLA Ops:
  8.6 69.4 %all-gather.5.cloned.1.call-done = bf16[2048,2368]{0,1:T(8,128)(2,1)} async-done(((bf16[512,2368]{0,1:T(8,128)(2,1)}), bf16[2048,2368]{0,1:T(8,128)(2,1)}) %all-gather.5.cloned.1.call-update) | async-done | bytes 9699344 | tf_op jit(solution)/shard_map/all_gather | solution.py:49
  83.7 368.1 %all-gather.3.cloned.1.call-done = bf16[2048,4736]{1,0:T(8,128)(2,1)} async-done(((bf16[256,4736]{1,0:T(8,128)(2,1)}), bf16[2048,4736]{1,0:T(8,128)(2,1)}) %all-gather.3.cloned.1.call-update) | async-done | bytes 19398672 | tf_op jit(solution)/shard_map/all_gather | solution.py:52
  460.2 59.7 %fusion.24 = (f32[4736]{0:T(1024)S(1)}, f32[4736,2368]{0,1:T(8,128)}) fusion(f32[2368]{0:T(1024)S(1)} %add_rsqrt_fusion.1, f32[4736]{0:T(1024)S(1)} %add_rsqrt_fusion, bf16[2048,2368]{0,1:T(8,128)(2,1)} %all-gather.5.cloned.1.call-done, bf16[2048,4736]{1,0:T(8,128)(2,1)} %all-gather.3.cloned.1.call-done), kind=kOutput, calls=%fused_computation.60 | convolution fusion | flops 45980872704 | bytes 74004736 | tf_op jit(solution)/shard_map/dot_general | solution.py:53
  525.2 17.3 %exponential_reduce_fusion.7 = f32[4736]{0:T(1024)S(1)} fusion(f32[4736,2368]{0,1:T(8,128)} %get-tuple-element.3, f32[4736]{0:T(1024)S(1)} %get-tuple-element.2), kind=kLoop, calls=%fused_computation.7 | loop fusion | flops 22424960 | bytes 44897280 | tf_op jit(solution)/shard_map/reduce_sum | solution.py:18
  556.0 33.5 %all-reduce = f32[4736]{0:T(1024)S(1)} all-reduce(f32[4736]{0:T(1024)S(1)} %subtract_dynamic-update-slice_fusion.7), channel_id=1, replica_groups=mesh['row'=4,'col'=8] {'col'}, use_global_device_ids=true, to_apply=%add | all-reduce | flops 4736 | bytes 37888
  589.5 14.8 %add_reduce_fusion.6 = f32[2368]{0:T(1024)S(1)} fusion(f32[4736,2368]{0,1:T(8,128)} %get-tuple-element.3, f32[4736]{0:T(1024)S(1)} %all-reduce), kind=kLoop, calls=%fused_computation.15 | loop fusion | flops 22427328 | bytes 44887808 | tf_op jit(solution)/shard_map/reduce_max | solution.py:33
  608.2 15.9 %exponential_reduce_fusion.6 = f32[2368]{0:T(1024)S(1)} fusion(f32[4736,2368]{0,1:T(8,128)} %get-tuple-element.3, f32[2368]{0:T(1024)S(1)} %add_reduce_fusion.6, f32[4736]{0:T(1024)S(1)} %all-reduce), kind=kLoop, calls=%fused_computation.6 | loop fusion | flops 33642176 | bytes 44897280 | tf_op jit(solution)/shard_map/reduce_sum | solution.py:34
  632.0 10.1 all-reduce.1
  642.1 16.4 %add_reduce_fusion.5 = f32[4736]{0:T(1024)S(1)} fusion(f32[4736,2368]{0,1:T(8,128)} %get-tuple-element.3, f32[2368]{0:T(1024)S(1)} %all-reduce.1), kind=kLoop, calls=%fused_computation.14 | loop fusion | flops 22424960 | bytes 44887808 | tf_op jit(solution)/shard_map/reduce_max | solution.py:17
  662.6 18.4 %exponential_reduce_fusion.5 = f32[4736]{0:T(1024)S(1)} fusion(f32[4736,2368]{0,1:T(8,128)} %get-tuple-element.3, f32[4736]{0:T(1024)S(1)} %add_reduce_fusion.5, f32[2368]{0:T(1024)S(1)} %all-reduce.1), kind=kLoop, calls=%fused_computation.5 | loop fusion | flops 33639808 | bytes 44906752 | tf_op jit(solution)/shard_map/reduce_sum | solution.py:18
  694.4 33.5 %all-reduce.2 = f32[4736]{0:T(1024)S(1)} all-reduce(f32[4736]{0:T(1024)S(1)} %subtract_dynamic-update-slice_fusion.5), channel_id=1, replica_groups=mesh['row'=4,'col'=8] {'col'}, use_global_device_ids=true, to_apply=%add.2 | all-reduce | flops 4736 | bytes 37888
  727.9 14.8 %add_reduce_fusion.4 = f32[2368]{0:T(1024)S(1)} fusion(f32[4736,2368]{0,1:T(8,128)} %get-tuple-element.3, f32[4736]{0:T(1024)S(1)} %all-reduce.2), kind=kLoop, calls=%fused_computation.13 | loop fusion | flops 22427328 | bytes 44887808 | tf_op jit(solution)/shard_map/reduce_max | solution.py:33
  746.6 15.9 %exponential_reduce_fusion.4 = f32[2368]{0:T(1024)S(1)} fusion(f32[4736,2368]{0,1:T(8,128)} %get-tuple-element.3, f32[2368]{0:T(1024)S(1)} %add_reduce_fusion.4, f32[4736]{0:T(1024)S(1)} %all-reduce.2), kind=kLoop, calls=%fused_computation.4 | loop fusion | flops 33642176 | bytes 44897280 | tf_op jit(solution)/shard_map/reduce_sum | solution.py:34
  780.5 16.4 %add_reduce_fusion.3 = f32[4736]{0:T(1024)S(1)} fusion(f32[4736,2368]{0,1:T(8,128)} %get-tuple-element.3, f32[2368]{0:T(1024)S(1)} %all-reduce.3), kind=kLoop, calls=%fused_computation.12 | loop fusion | flops 22424960 | bytes 44887808 | tf_op jit(solution)/shard_map/reduce_max | solution.py:17
  801.0 18.4 %exponential_reduce_fusion.3 = f32[4736]{0:T(1024)S(1)} fusion(f32[4736,2368]{0,1:T(8,128)} %get-tuple-element.3, f32[4736]{0:T(1024)S(1)} %add_reduce_fusion.3, f32[2368]{0:T(1024)S(1)} %all-reduce.3), kind=kLoop, calls=%fused_computation.3 | loop fusion | flops 33639808 | bytes 44906752 | tf_op jit(solution)/shard_map/reduce_sum | solution.py:18
  832.8 33.5 %all-reduce.4 = f32[4736]{0:T(1024)S(1)} all-reduce(f32[4736]{0:T(1024)S(1)} %subtract_dynamic-update-slice_fusion.3), channel_id=1, replica_groups=mesh['row'=4,'col'=8] {'col'}, use_global_device_ids=true, to_apply=%add.4 | all-reduce | flops 4736 | bytes 37888
  866.2 14.8 %add_reduce_fusion.2 = f32[2368]{0:T(1024)S(1)} fusion(f32[4736,2368]{0,1:T(8,128)} %get-tuple-element.3, f32[4736]{0:T(1024)S(1)} %all-reduce.4), kind=kLoop, calls=%fused_computation.11 | loop fusion | flops 22427328 | bytes 44887808 | tf_op jit(solution)/shard_map/reduce_max | solution.py:33
  885.2 15.9 %exponential_reduce_fusion.2 = f32[2368]{0:T(1024)S(1)} fusion(f32[4736,2368]{0,1:T(8,128)} %get-tuple-element.3, f32[2368]{0:T(1024)S(1)} %add_reduce_fusion.2, f32[4736]{0:T(1024)S(1)} %all-reduce.4), kind=kLoop, calls=%fused_computation.2 | loop fusion | flops 33642176 | bytes 44897280 | tf_op jit(solution)/shard_map/reduce_sum | solution.py:34
  919.0 16.4 %add_reduce_fusion.1 = f32[4736]{0:T(1024)S(1)} fusion(f32[4736,2368]{0,1:T(8,128)} %get-tuple-element.3, f32[2368]{0:T(1024)S(1)} %all-reduce.5), kind=kLoop, calls=%fused_computation.10 | loop fusion | flops 22424960 | bytes 44887808 | tf_op jit(solution)/shard_map/reduce_max | solution.py:17
  939.5 18.4 %exponential_reduce_fusion.1 = f32[4736]{0:T(1024)S(1)} fusion(f32[4736,2368]{0,1:T(8,128)} %get-tuple-element.3, f32[4736]{0:T(1024)S(1)} %add_reduce_fusion.1, f32[2368]{0:T(1024)S(1)} %all-reduce.5), kind=kLoop, calls=%fused_computation.1 | loop fusion | flops 33639808 | bytes 44906752 | tf_op jit(solution)/shard_map/reduce_sum | solution.py:18
  971.3 33.5 %all-reduce.6 = f32[4736]{0:T(1024)S(1)} all-reduce(f32[4736]{0:T(1024)S(1)} %subtract_dynamic-update-slice_fusion.1), channel_id=1, replica_groups=mesh['row'=4,'col'=8] {'col'}, use_global_device_ids=true, to_apply=%add.6 | all-reduce | flops 4736 | bytes 37888
  1004.8 14.8 %add_reduce_fusion = f32[2368]{0:T(1024)S(1)} fusion(f32[4736,2368]{0,1:T(8,128)} %get-tuple-element.3, f32[4736]{0:T(1024)S(1)} %all-reduce.6), kind=kLoop, calls=%fused_computation.9 | loop fusion | flops 22427328 | bytes 44887808 | tf_op jit(solution)/shard_map/reduce_max | solution.py:33
  1023.5 15.9 %exponential_reduce_fusion = f32[2368]{0:T(1024)S(1)} fusion(f32[4736,2368]{0,1:T(8,128)} %get-tuple-element.3, f32[2368]{0:T(1024)S(1)} %add_reduce_fusion, f32[4736]{0:T(1024)S(1)} %all-reduce.6), kind=kLoop, calls=%fused_computation | loop fusion | flops 33642176 | bytes 44897280 | tf_op jit(solution)/shard_map/reduce_sum | solution.py:34
  1047.3 10.7 %all-reduce.7 = f32[2368]{0:T(1024)} all-reduce(f32[2368]{0:T(1024)S(1)} %subtract_dynamic-update-slice_fusion), channel_id=1, replica_groups=mesh['row'=4,'col'=8] {'row'}, use_global_device_ids=true, to_apply=%add.7 | all-reduce | flops 2368 | bytes 18944
  (98 shorter events, 153.0 us)
Async XLA Ops:
  7.2 70.8 %all-gather.5.cloned.1.call-start = ((), (), s32[]{:S(2)}) async-start(), calls=%async_computation.17 | async-start | bytes 12124160 | tf_op jit(solution)/shard_map/all_gather | solution.py:49
  7.9 443.9 %all-gather.3.cloned.1.call-start = ((), (), s32[]{:S(2)}) async-start(), calls=%async_computation.16 | async-start | bytes 21823488 | tf_op jit(solution)/shard_map/all_gather | solution.py:52
  519.9 29.3 %copy-start.2 = (u32[32]{0:T(128)S(1)}, u32[32]{0:T(128)}, u32[]{:S(2)}) copy-start(u32[32]{0:T(128)} %constant.20) | copy-start | bytes 388
  520.6 22.6 %all-to-all-start = ((f32[8,1,592]{2,1,0:T(1,128)}), f32[8,1,592]{2,1,0:T(1,128)S(1)}, u32[]{:S(2)}, u32[]{:S(2)}) async-start(f32[8,1,592]{2,1,0:T(1,128)} %all_to_all.128), calls=%async_computation | async-start | bytes 40960 | tf_op jit(solution)/shard_map/all_to_all | solution.py:21
  543.3 12.6 %all-to-all-start.1 = ((f32[8,1,592]{2,1,0:T(1,128)}), f32[8,1,592]{2,1,0:T(1,128)S(1)}, u32[]{:S(2)}, u32[]{:S(2)}) async-start(f32[8,1,592]{2,1,0:T(1,128)} %all_to_all.130), calls=%async_computation.1 | async-start | bytes 40960 | tf_op jit(solution)/shard_map/all_to_all | solution.py:24
  589.5 38.5 %copy-start.1 = (u32[32]{0:T(128)S(1)}, u32[32]{0:T(128)}, u32[]{:S(2)}) copy-start(u32[32]{0:T(128)} %constant.25) | copy-start | bytes 388
  605.0 19.8 %all-to-all-start.2 = ((f32[4,1,592]{2,1,0:T(1,128)}), f32[4,1,592]{2,1,0:T(1,128)S(1)}, u32[]{:S(2)}, u32[]{:S(2)}) async-start(f32[4,1,592]{2,1,0:T(1,128)} %all_to_all.134), calls=%async_computation.2 | async-start | bytes 20480 | tf_op jit(solution)/shard_map/all_to_all | solution.py:37
  624.8 7.1 all-to-all-start.3
  659.3 22.5 %all-to-all-start.4 = ((f32[8,1,592]{2,1,0:T(1,128)}), f32[8,1,592]{2,1,0:T(1,128)S(1)}, u32[]{:S(2)}, u32[]{:S(2)}) async-start(f32[8,1,592]{2,1,0:T(1,128)} %all_to_all.140), calls=%async_computation.4 | async-start | bytes 40960 | tf_op jit(solution)/shard_map/all_to_all | solution.py:21
  681.7 12.5 %all-to-all-start.5 = ((f32[8,1,592]{2,1,0:T(1,128)}), f32[8,1,592]{2,1,0:T(1,128)S(1)}, u32[]{:S(2)}, u32[]{:S(2)}) async-start(f32[8,1,592]{2,1,0:T(1,128)} %all_to_all.142), calls=%async_computation.5 | async-start | bytes 40960 | tf_op jit(solution)/shard_map/all_to_all | solution.py:24
  743.3 19.8 %all-to-all-start.6 = ((f32[4,1,592]{2,1,0:T(1,128)}), f32[4,1,592]{2,1,0:T(1,128)S(1)}, u32[]{:S(2)}, u32[]{:S(2)}) async-start(f32[4,1,592]{2,1,0:T(1,128)} %all_to_all.146), calls=%async_computation.6 | async-start | bytes 20480 | tf_op jit(solution)/shard_map/all_to_all | solution.py:37
  763.1 7.1 all-to-all-start.7
  797.6 22.5 %all-to-all-start.8 = ((f32[8,1,592]{2,1,0:T(1,128)}), f32[8,1,592]{2,1,0:T(1,128)S(1)}, u32[]{:S(2)}, u32[]{:S(2)}) async-start(f32[8,1,592]{2,1,0:T(1,128)} %all_to_all.152), calls=%async_computation.8 | async-start | bytes 40960 | tf_op jit(solution)/shard_map/all_to_all | solution.py:21
  820.1 12.5 %all-to-all-start.9 = ((f32[8,1,592]{2,1,0:T(1,128)}), f32[8,1,592]{2,1,0:T(1,128)S(1)}, u32[]{:S(2)}, u32[]{:S(2)}) async-start(f32[8,1,592]{2,1,0:T(1,128)} %all_to_all.154), calls=%async_computation.9 | async-start | bytes 40960 | tf_op jit(solution)/shard_map/all_to_all | solution.py:24
  881.7 20.0 %all-to-all-start.10 = ((f32[4,1,592]{2,1,0:T(1,128)}), f32[4,1,592]{2,1,0:T(1,128)S(1)}, u32[]{:S(2)}, u32[]{:S(2)}) async-start(f32[4,1,592]{2,1,0:T(1,128)} %all_to_all.158), calls=%async_computation.10 | async-start | bytes 20480 | tf_op jit(solution)/shard_map/all_to_all | solution.py:37
  901.7 7.0 all-to-all-start.11
  936.2 22.5 %all-to-all-start.12 = ((f32[8,1,592]{2,1,0:T(1,128)}), f32[8,1,592]{2,1,0:T(1,128)S(1)}, u32[]{:S(2)}, u32[]{:S(2)}) async-start(f32[8,1,592]{2,1,0:T(1,128)} %all_to_all.164), calls=%async_computation.12 | async-start | bytes 40960 | tf_op jit(solution)/shard_map/all_to_all | solution.py:21
  958.6 12.5 %all-to-all-start.13 = ((f32[8,1,592]{2,1,0:T(1,128)}), f32[8,1,592]{2,1,0:T(1,128)S(1)}, u32[]{:S(2)}, u32[]{:S(2)}) async-start(f32[8,1,592]{2,1,0:T(1,128)} %all_to_all.166), calls=%async_computation.13 | async-start | bytes 40960 | tf_op jit(solution)/shard_map/all_to_all | solution.py:24
  1004.8 34.6 %copy-start = (f32[4736]{0:T(1024)}, f32[4736]{0:T(1024)S(1)}, u32[]{:S(2)}) copy-start(f32[4736]{0:T(1024)S(1)} %all-reduce.6) | copy-start | bytes 56836
  1020.3 19.8 %all-to-all-start.14 = ((f32[4,1,592]{2,1,0:T(1,128)}), f32[4,1,592]{2,1,0:T(1,128)S(1)}, u32[]{:S(2)}, u32[]{:S(2)}) async-start(f32[4,1,592]{2,1,0:T(1,128)} %all_to_all.170), calls=%async_computation.14 | async-start | bytes 20480 | tf_op jit(solution)/shard_map/all_to_all | solution.py:37
  1040.1 7.1 all-to-all-start.15
Sparse Core Ops, SparseCore 0:
  9.5 68.4 all-gather.4
  79.5 372.2 all-gather.2
where the time goes:
time: 1070 us; the launch traced here: 1060 us
  waiting for transfers between devices  478 us (45%)
  other arithmetic  260 us (24%)
  blocking collectives  175 us (16%)
  starting transfers between devices  64.7 us (6%)
  matrix products  59.7 us (6%)
  between operations  15.7 us (1%)
  local copies, waits for them, and re-layouts  12.3 us (1%)
    all_gather x1, waiting for transfers between devices, shards(): segment = lax.all_gather(first_acts, 'col', axis=0, tiled=True)  368 us
    unnamed x8, blocking collectives  175 us
    reduce_sum x4, other arithmetic, row_lse(): totals = jnp.sum(jnp.exp(scores - highest[:, None]), 1)  72.5 us
    all_gather x1, waiting for transfers between devices, shards(): full_second = lax.all_gather(second_acts, 'row', axis=0, tiled=True)  69.4 us
    reduce_sum x4, other arithmetic, col_lse(): totals = jnp.sum(jnp.exp(scores - highest[None, :]), 0)  63.5 us
    dot_general x1, matrix products, shards(): lax.dot_general(segment, full_second, (((0,), (0,)), ((), ())), preferred...  59.7 us
    reduce_max x4, other arithmetic, col_lse(): highest = jnp.max(scores, 0)  59.1 us
    reduce_max x3, other arithmetic, row_lse(): highest = jnp.max(scores, 1)  49.3 us
  transfers between devices with their start and end apart: 18, of which 10 were waited for; matrix products, arithmetic and copies ran while one was open for 13% of the time, Pallas kernels for 0%

commit v1 on v0

v1 whole, which is shorter than its diff:
```python
import functools
import math

import jax
import jax.numpy as jnp
from jax import lax
from jax.experimental import pallas as pl
from jax.experimental.pallas import tpu as pltpu
from jax.sharding import PartitionSpec as P

ITERS = 4
ENTROPY_SCALE = 0.004
LOG2E = 1.0 / math.log(2.0)
LN2 = math.log(2.0)
SHIFT = 58.0
LOW = -1e30
LANES = 128
MESH = pl.DeviceIdType.MESH


def round_up(value, unit):
    return -(-value // unit) * unit


def kernel(
    rows, cols, total, samples,
    a_hbm, b_ref, row_out, col_out,
    acc, abuf, f_vec, g_vec, a_vec, b_vec, inv_b, col_max, col_sum,
    send_r0, recv_r0, send_r, recv_r, send_c0, recv_c0, send_c, recv_c,
    load_sem, rs0, rr0, rs, rr, cs0, cr0, cs, cr,
):
    n_row, n_col = lax.axis_size("row"), lax.axis_size("col")
    my_row, my_col = lax.axis_index("row"), lax.axis_index("col")
    chunks, rows_pad, depth = a_hbm.shape
    cols_pad = b_ref.shape[1]
    tile = abuf.shape[1]
    share = -math.log(total) * LOG2E
    blocks = rows_pad // LANES
    lane_tiles = cols_pad // LANES

    barrier = pltpu.get_barrier_semaphore()
    for axis, me, n in (("row", my_row, n_row), ("col", my_col, n_col)):
        for d in range(1, n):
            pl.semaphore_signal(
                barrier, inc=1, device_id={axis: lax.rem(me + d, n)}, device_id_type=MESH
            )
    pl.semaphore_wait(barrier, n_row + n_col - 2)

    def exchange(axis, me, n, send, recv, ssem, rsem):
        copies = []
        for d in range(1, n):
            copy = pltpu.make_async_remote_copy(
                src_ref=send,
                dst_ref=recv.at[d - 1],
                send_sem=ssem.at[d - 1],
                recv_sem=rsem.at[d - 1],
                device_id={axis: lax.rem(me + d, n)},
                device_id_type=MESH,
            )
            copy.start()
            copies.append(copy)
        for copy in copies:
            copy.wait()

    def load(index, start, size, slot):
        return [
            pltpu.make_async_copy(
                a_hbm.at[c, pl.ds(start, size), :],
                abuf.at[slot, pl.ds(0, size), pl.ds(c * depth, depth)],
                load_sem.at[slot, c],
            )
            for c in range(chunks)
        ]

    full = rows_pad // tile
    tail = rows_pad - full * tile

    if full:
        for copy in load(0, 0, tile, 0):
            copy.start()

    def square_step(i, unused):
        part = b_ref[pl.ds(pl.multiple_of(i * 32, 32), 32), :].astype(jnp.float32)
        sq = part * part
        col_sum[...] += sq[0:8] + sq[8:16] + sq[16:24] + sq[24:32]
        return unused

    col_sum[...] = jnp.zeros_like(col_sum)
    lax.fori_loop(0, samples // 32, square_step, 0)
    sq_b = jnp.sum(col_sum[...], 0, keepdims=True)
    inv_b[...] = (LOG2E / (samples * ENTROPY_SCALE)) / jnp.sqrt(sq_b / samples + 1e-6)

    n_tile = 1024
    n_edges = [(s, min(s + n_tile, cols_pad)) for s in range(0, cols_pad, n_tile)]

    def matmul_tile(start, size, slot):
        a_tile = abuf.at[slot]
        sq = jnp.zeros((size, LANES), jnp.float32)
        for k in range(samples // LANES):
            w = a_tile[0:size, k * LANES:(k + 1) * LANES].astype(jnp.float32)
            sq = sq + w * w
        inv_a = 1.0 / jnp.sqrt(jnp.sum(sq, 1, keepdims=True) / samples + 1e-6)
        for lo, hi in n_edges:
            prod = jnp.dot(
                a_tile[0:size, :], b_ref[:, lo:hi], preferred_element_type=jnp.float32
            )
            x = prod * inv_a * inv_b[:, lo:hi]
            if hi > cols:
                lane = lax.broadcasted_iota(jnp.int32, (size, hi - lo), 1) + lo
                x = jnp.where(lane < cols, x, LOW)
            acc[pl.ds(start, size), lo:hi] = x

    def row_stats(i, unused):
        at = pl.ds(pl.multiple_of(i * LANES, LANES), LANES)
        top = acc[at, 0:LANES]
        for k in range(1, lane_tiles):
            top = jnp.maximum(top, acc[at, k * LANES:(k + 1) * LANES])
        top = jnp.broadcast_to(jnp.max(top, 1, keepdims=True), (LANES, LANES))
        part = jnp.zeros((LANES, LANES), jnp.float32)
        for k in range(lane_tiles):
            part = part + jnp.exp2(acc[at, k * LANES:(k + 1) * LANES] - top)
        send_r0[0:1, at] = top.T[0:1]
        send_r0[1:2, at] = jnp.sum(part.T, 0, keepdims=True)
        return unused

    def tile_step(t, unused):
        slot = lax.rem(t, 2)
        start = pl.multiple_of(t * tile, tile)
        for copy in load(t, start, tile, slot):
            copy.wait()

        @pl.when(t + 1 < full)
        def _():
            for copy in load(t + 1, pl.multiple_of((t + 1) * tile, tile), tile, 1 - slot):
                copy.start()

        matmul_tile(start, tile, slot)
        lax.fori_loop(t * (tile // LANES), (t + 1) * (tile // LANES), row_stats, 0)
        return unused

    if full:
        lax.fori_loop(0, full, tile_step, 0)
    if tail:
        slot = full % 2
        copies = load(full, full * tile, tail, slot)
        for copy in copies:
            copy.start()
        for copy in copies:
            copy.wait()
        matmul_tile(full * tile, tail, slot)
        lax.fori_loop(full * (tile // LANES), blocks, row_stats, 0)

    def merge(send, recv, n):
        parts = [send[...]] + [recv[d] for d in range(n - 1)]
        top = parts[0][0:1]
        for p in parts[1:]:
            top = jnp.maximum(top, p[0:1])
        acc_sum = jnp.zeros_like(top)
        for p in parts:
            acc_sum = acc_sum + p[1:2] * jnp.exp2(p[0:1] - top)
        return share - (top + jnp.log(acc_sum) * LOG2E)

    exchange("col", my_col, n_col, send_r0, recv_r0, rs0, rr0)
    first_f = merge(send_r0, recv_r0, n_col)
    if rows_pad != rows:
        first_f = jnp.where(
            lax.broadcasted_iota(jnp.int32, (1, rows_pad), 1) < rows, first_f, LOW
        )
    f_vec[...] = first_f

    def spread(ref, at):
        return jnp.broadcast_to(ref[:, at], (LANES, LANES)).T

    def fold(value, op):
        parts = [value[8 * s:8 * s + 8] for s in range(value.shape[0] // 8)]
        while len(parts) > 1:
            parts = [op(parts[i], parts[i + 1]) for i in range(0, len(parts), 2)]
        return parts[0]

    col_max[...] = jnp.full(col_max.shape, 2 * LOW, jnp.float32)
    col_sum[...] = jnp.zeros_like(col_sum)

    def first_col(i, unused):
        at = pl.ds(pl.multiple_of(i * LANES, LANES), LANES)
        f_rep = spread(f_vec, at)
        for k in range(lane_tiles):
            lanes = slice(k * LANES, (k + 1) * LANES)
            y = acc[at, lanes] + f_rep
            old = col_max[:, lanes]
            new = jnp.maximum(old, fold(y, jnp.maximum))
            e = jnp.exp2(y - jnp.concatenate([new] * (LANES // 8), 0))
            col_sum[:, lanes] = col_sum[:, lanes] * jnp.exp2(old - new) + fold(e, jnp.add)
            col_max[:, lanes] = new
        return unused

    lax.fori_loop(0, blocks, first_col, 0)
    top = jnp.max(col_max[...], 0, keepdims=True)
    send_c0[0:1, :] = top
    send_c0[1:2, :] = jnp.sum(col_sum[...] * jnp.exp2(col_max[...] - top), 0, keepdims=True)
    exchange("row", my_row, n_row, send_c0, recv_c0, cs0, cr0)
    first_g = merge(send_c0, recv_c0, n_row)
    if cols_pad != cols:
        first_g = jnp.where(
            lax.broadcasted_iota(jnp.int32, (1, cols_pad), 1) < cols, first_g, 0.0
        )
    g_vec[...] = first_g

    gain = 2.0 ** SHIFT / total

    for step in range(ITERS - 1):

        def row_pass(i, unused):
            at = pl.ds(pl.multiple_of(i * LANES, LANES), LANES)
            part = jnp.zeros((LANES, LANES), jnp.float32)
            if step == 0:
                f_rep = spread(f_vec, at) + SHIFT
            for k in range(lane_tiles):
                lanes = slice(k * LANES, (k + 1) * LANES)
                if step == 0:
                    p = jnp.exp2(acc[at, lanes] + f_rep + g_vec[:, lanes])
                    acc[at, lanes] = p
                    part = part + p
                else:
                    part = part + acc[at, lanes] * b_vec[:, lanes]
            send_r[step, 0:1, at] = jnp.sum(part.T, 0, keepdims=True)
            return unused

        lax.fori_loop(0, blocks, row_pass, 0)
        exchange("col", my_col, n_col, send_r.at[step], recv_r.at[step], rs.at[step], rr.at[step])
        merged = send_r[step]
        for d in range(n_col - 1):
            merged = merged + recv_r[step, d]
        scale_a = gain / merged
        if rows_pad != rows:
            scale_a = jnp.where(
                lax.broadcasted_iota(jnp.int32, (1, rows_pad), 1) < rows, scale_a, 0.0
            )
        a_vec[...] = scale_a
        col_sum[...] = jnp.zeros_like(col_sum)

        def col_pass(i, unused):
            at = pl.ds(pl.multiple_of(i * LANES, LANES), LANES)
            a_rep = spread(a_vec, at)
            for k in range(lane_tiles):
                lanes = slice(k * LANES, (k + 1) * LANES)
                col_sum[:, lanes] += fold(acc[at, lanes] * a_rep, jnp.add)
            return unused

        lax.fori_loop(0, blocks, col_pass, 0)
        send_c[step] = jnp.sum(col_sum[...], 0, keepdims=True)
        exchange("row", my_row, n_row, send_c.at[step], recv_c.at[step], cs.at[step], cr.at[step])
        merged = send_c[step]
        for d in range(n_row - 1):
            merged = merged + recv_c[step, d]
        scale_b = gain / merged
        if cols_pad != cols:
            scale_b = jnp.where(
                lax.broadcasted_iota(jnp.int32, (1, cols_pad), 1) < cols, scale_b, 1.0
            )
        b_vec[...] = scale_b

    row_out[...] = f_vec[...] * LN2 + jnp.log(a_vec[...])
    col_out[...] = g_vec[...] * LN2 + jnp.log(b_vec[...])


def shards(first_acts, second_acts):
    rows, cols = first_acts.shape[1], second_acts.shape[1]
    n_row, n_col = lax.axis_size("row"), lax.axis_size("col")
    samples = second_acts.shape[0] * n_row
    rows_pad, cols_pad = round_up(rows, LANES), round_up(cols, LANES)
    first = jnp.pad(first_acts, ((0, 0), (0, rows_pad - rows)))
    second = jnp.pad(second_acts, ((0, 0), (0, cols_pad - cols)))
    b_full = lax.all_gather(second, "row", axis=0, tiled=True)
    if first.shape[0] % LANES == 0:
        a_full = lax.all_gather(first.T, "col", axis=0, tiled=False)
    else:
        a_full = lax.all_gather(first, "col", axis=0, tiled=True).T[None]
    chunks = a_full.shape[0]
    tile = 512
    rest = ITERS - 1
    f32 = jnp.float32
    vmem = pltpu.VMEM
    dma = pltpu.SemaphoreType.DMA
    row_out, col_out = pl.pallas_call(
        functools.partial(kernel, rows, cols, rows * n_row, samples),
        out_shape=(
            jax.ShapeDtypeStruct((1, rows_pad), f32),
            jax.ShapeDtypeStruct((1, cols_pad), f32),
        ),
        in_specs=[pl.BlockSpec(memory_space=pl.ANY), pl.BlockSpec(memory_space=vmem)],
        out_specs=(pl.BlockSpec(memory_space=vmem),) * 2,
        scratch_shapes=[
            vmem((rows_pad, cols_pad), f32),
            vmem((2, tile, samples), jnp.bfloat16),
            vmem((1, rows_pad), f32),
            vmem((1, cols_pad), f32),
            vmem((1, rows_pad), f32),
            vmem((1, cols_pad), f32),
            vmem((1, cols_pad), f32),
            vmem((8, cols_pad), f32),
            vmem((8, cols_pad), f32),
            vmem((2, rows_pad), f32),
            vmem((n_col - 1, 2, rows_pad), f32),
            vmem((rest, 1, rows_pad), f32),
            vmem((rest, n_col - 1, 1, rows_pad), f32),
            vmem((2, cols_pad), f32),
            vmem((n_row - 1, 2, cols_pad), f32),
            vmem((rest, 1, cols_pad), f32),
            vmem((rest, n_row - 1, 1, cols_pad), f32),
            dma((2, chunks)),
            dma((n_col - 1,)),
            dma((n_col - 1,)),
            dma((rest, n_col - 1)),
            dma((rest, n_col - 1)),
            dma((n_row - 1,)),
            dma((n_row - 1,)),
            dma((rest, n_row - 1)),
            dma((rest, n_row - 1)),
        ],
        compiler_params=pltpu.CompilerParams(
            collective_id=0, has_side_effects=True, vmem_limit_bytes=67043328
        ),
    )(a_full, b_full)
    return row_out[0, :rows], col_out[0, :cols]


def solution(mesh):
    return jax.shard_map(
        shards,
        mesh=mesh,
        in_specs=(P("col", "row"), P("row", "col")),
        out_specs=(P("row"), P("col")),
        check_vma=False,
    )
```

time: 1070 us -> 632 us (0.59)
  other arithmetic: 260 us -> 1.37 us
  blocking collectives: 175 us -> 0 us
  Pallas kernels: 0 us -> 168 us
  starting transfers between devices: 64.7 us -> 0.08 us
  waiting for transfers between devices: 478 us -> 416 us
  matrix products: 59.7 us -> 0 us
  local copies, waits for them, and re-layouts: 12.3 us -> 31 us
    unnamed x8 -> x0, blocking collectives: 175 us -> none
    pallas_call x0 -> x1, Pallas kernels: none -> 168 us  [shards(): pl.pallas_call(functools.partial(kernel, rows, cols, rows * n_row, sample...]
    reduce_sum x18 -> x0, other arithmetic: 150 us -> none  [the longest x4 72.5 us: row_lse(): totals = jnp.sum(jnp.exp(scores - highest[:, None]), 1)]
    reduce_max x15 -> x0, other arithmetic: 109 us -> none  [the longest x4 59.1 us: col_lse(): highest = jnp.max(scores, 0)]
    all_to_all x16 -> x0, starting transfers between devices: 64.6 us -> none  [the longest x4 23.8 us: row_lse(): lax.all_to_all(totals.reshape(members, -1), 'col', split_axis=0, concat_a...]
    dot_general x1 -> x0, matrix products: 59.7 us -> none  [shards(): lax.dot_general(segment, full_second, (((0,), (0,)), ((), ())), preferred...]
    all_to_all x16 -> x0, waiting for transfers between devices: 38.9 us -> none  [the longest x4 25.1 us: row_lse(): lax.all_to_all(totals.reshape(members, -1), 'col', split_axis=0, concat_a...]
    all_gather x0 -> x1, local copies, waits for them, and re-layouts: none -> 24.9 us  [shards(): a_full = lax.all_gather(first.T, 'col', axis=0, tiled=False)]
  transfers between devices with their start and end apart: 18 -> 2, of which waited for: 10 -> 2; matrix products, arithmetic and copies ran while one was open for 13% -> 5% of each run, Pallas kernels for 0% -> 0%
where the time goes in v1:
time: 632 us; the launch traced here: 631 us
  waiting for transfers between devices  416 us (66%)
  Pallas kernels  168 us (27%)
  local copies, waits for them, and re-layouts  31 us (5%)
  between operations  14.1 us (2%)
    all_gather x1, waiting for transfers between devices, shards(): a_full = lax.all_gather(first.T, 'col', axis=0, tiled=False)  372 us
    pallas_call x1, Pallas kernels, shards(): pl.pallas_call(functools.partial(kernel, rows, cols, rows * n_row, sample...  168 us
    all_gather x1, waiting for transfers between devices, shards(): b_full = lax.all_gather(second, 'row', axis=0, tiled=True)  43.8 us
    all_gather x1, local copies, waits for them, and re-layouts, shards(): a_full = lax.all_gather(first.T, 'col', axis=0, tiled=False)  24.9 us
  transfers between devices with their start and end apart: 2, of which 2 were waited for; matrix products, arithmetic and copies ran while one was open for 5% of the time, Pallas kernels for 0%

profile of v1, /device:TPU:0, one launch (start us, length us, event | category | flops | bytes accessed | tf_op | source)
XLA Modules:
  0.0 631.2 jit_solution(12929132205690478932)
XLA Ops:
  7.2 0.0 all-gather.6.cloned.1.call-start
  7.2 0.7 all-gather.6.cloned.1.call-update
  7.9 0.0 all-gather.4.cloned.1.call-start
  7.9 3.1 copy.5
  11.0 1.6 pad.4
  12.7 0.0 all-gather.4.cloned.1.call-update
  12.7 371.8 %all-gather.6.cloned.1.call-done = bf16[37888,256]{0,1:T(8,128)(2,1)} async-done(((bf16[4736,256]{0,1:T(8,128)(2,1)}), bf16[37888,256]{0,1:T(8,128)(2,1)}) %all-gather.6.cloned.1.call-update) | async-done | bytes 19398672 | tf_op jit(solution)/shard_map/all_gather | solution.py:275
  384.5 24.9 %copy.4 = bf16[37888,256]{1,0:T(8,128)(2,1)} copy(bf16[37888,256]{0,1:T(8,128)(2,1)} %all-gather.6.cloned.1.call-done) | data formatting | bytes 38797312 | tf_op jit(solution)/shard_map/all_gather | solution.py:275
  409.4 43.8 %all-gather.4.cloned.1.call-done.b_ref = bf16[2048,2432]{1,0:T(8,128)(2,1)} async-done(((bf16[512,2432]{1,0:T(8,128)(2,1)}), bf16[2048,2432]{1,0:T(8,128)(2,1)}) %all-gather.4.cloned.1.call-update) | async-done | bytes 9961488 | tf_op jit(solution)/shard_map/all_gather | solution.py:273
  453.3 168.4 %shard_map.41 = (f32[1,4736]{1,0:T(1,128)}, f32[1,2432]{1,0:T(1,128)}) custom-call(bf16[8,4736,256]{2,1,0:T(8,128)(2,1)} %bitcast.2, bf16[2048,2432]{1,0:T(8,128)(2,1)} %all-gather.4.cloned.1.call-done.b_ref), custom_call_target="tpu_custom_call" | custom-call | tf_op jit(solution)/shard_map/pallas_call | solution.py:284
  621.7 1.3 slice_reduce_fusion
  623.0 1.4 reduce
Async XLA Ops:
  7.2 377.3 %all-gather.6.cloned.1.call-start = ((), (), s32[]{:S(2)}) async-start(), calls=%async_computation.1 | async-start | bytes 21823488 | tf_op jit(solution)/shard_map/all_gather | solution.py:275
  7.9 445.4 %all-gather.4.cloned.1.call-start = ((), (), s32[]{:S(2)}) async-start(), calls=%async_computation | async-start | bytes 12451840 | tf_op jit(solution)/shard_map/all_gather | solution.py:273
Sparse Core Ops, SparseCore 0:
  9.5 374.9 all-gather.5
  386.1 67.1 all-gather.3

commit v2 on v1

--- a/solution.py
+++ b/solution.py
@@ -23,17 +23,19 @@
 
 
 def kernel(
-    rows, cols, total, samples,
-    a_hbm, b_ref, row_out, col_out,
+    rows, cols, total, samples, tile, remote,
+    a_hbm, b_hbm, row_out, col_out, a_full, b_ref,
     acc, abuf, f_vec, g_vec, a_vec, b_vec, inv_b, col_max, col_sum,
     send_r0, recv_r0, send_r, recv_r, send_c0, recv_c0, send_c, recv_c,
     load_sem, rs0, rr0, rs, rr, cs0, cr0, cs, cr,
+    own_sem, ga_s, ga_r, gb_s, gb_r,
 ):
     n_row, n_col = lax.axis_size("row"), lax.axis_size("col")
     my_row, my_col = lax.axis_index("row"), lax.axis_index("col")
-    chunks, rows_pad, depth = a_hbm.shape
+    rows_pad, depth = a_hbm.shape[1:]
+    chunks = samples // depth
     cols_pad = b_ref.shape[1]
-    tile = abuf.shape[1]
+    b_depth = b_hbm.shape[0]
     share = -math.log(total) * LOG2E
     blocks = rows_pad // LANES
     lane_tiles = cols_pad // LANES
@@ -62,22 +64,123 @@
         for copy in copies:
             copy.wait()
 
-    def load(index, start, size, slot):
-        return [
-            pltpu.make_async_copy(
-                a_hbm.at[c, pl.ds(start, size), :],
-                abuf.at[slot, pl.ds(0, size), pl.ds(c * depth, depth)],
-                load_sem.at[slot, c],
-            )
-            for c in range(chunks)
-        ]
-
     full = rows_pad // tile
     tail = rows_pad - full * tile
 
-    if full:
-        for copy in load(0, 0, tile, 0):
+    def relay(axis, me, n, src_of, dst_of, ssem, rsem):
+        outer = n // 2
+        mine_o, mine_i = me // 2, lax.rem(me, 2)
+
+        def index(d, inner):
+            return lax.rem(mine_o + d + outer, outer) * 2 + inner
+
+        def copy(src, dst, slot, target):
+            return pltpu.make_async_remote_copy(
+                src_ref=src,
+                dst_ref=dst,
+                send_sem=ssem(slot),
+                recv_sem=rsem(slot),
+                device_id={axis: target},
+                device_id_type=MESH,
+            )
+
+        partner = index(0, 1 - mine_i)
+        own = [
+            copy(src_of(), dst_of(me), d, index(d, mine_i)) for d in range(1, outer)
+        ]
+        own.append(copy(src_of(), dst_of(me), 0, partner))
+        passed = []
+        for d in range(1, outer):
+            source = index(-d, mine_i)
+            passed.append(copy(dst_of(source), dst_of(source), outer + d - 1, partner))
+        return own, passed
+
+    def a_relay(t, start, size):
+        return relay(
+            "col", my_col, n_col,
+            lambda: a_hbm.at[0, pl.ds(start, size), :],
+            lambda c: a_full.at[c, pl.ds(start, size), :],
+            lambda k: ga_s.at[t, k],
+            lambda k: ga_r.at[t, k],
+        )
+
+    def b_relay():
+        return relay(
+            "row", my_row, n_row,
+            lambda: b_hbm,
+            lambda c: b_ref.at[pl.ds(pl.multiple_of(c * b_depth, b_depth), b_depth), :],
+            lambda k: gb_s.at[k],
+            lambda k: gb_r.at[k],
+        )
+
+    def over_tiles(step):
+        if full:
+            lax.fori_loop(
+                0, full, lambda t, u: (step(t, pl.multiple_of(t * tile, tile), tile), u)[1], 0
+            )
+        if tail:
+            step(full, full * tile, tail)
+
+    def send_tile(t, start, size):
+        for copy in a_relay(t, start, size)[0]:
             copy.start()
+
+    def pass_tile(t, start, size):
+        own, passed = a_relay(t, start, size)
+        for arrived, onward in zip(own, passed):
+            arrived.wait_recv()
+            onward.start()
+
+    def wait_tile(t, start, size):
+        own, passed = a_relay(t, start, size)
+        own[-1].wait_recv()
+        for copy in passed:
+            copy.wait_recv()
+
+    def close_tile(t, start, size):
+        own, passed = a_relay(t, start, size)
+        for copy in own + passed:
+            copy.wait_send()
+
+    if remote:
+        base = pl.multiple_of(my_row * b_depth, b_depth)
+    else:
+        base = 0
+    own_b = pltpu.make_async_copy(b_hbm, b_ref.at[pl.ds(base, b_depth), :], own_sem)
+    own_b.start()
+    if remote:
+        b_own, b_passed = b_relay()
+        for copy in b_own:
+            copy.start()
+        over_tiles(send_tile)
+        for arrived, onward in zip(b_own, b_passed):
+            arrived.wait_recv()
+            onward.start()
+        b_own[-1].wait_recv()
+        for copy in b_passed:
+            copy.wait_recv()
+    own_b.wait()
+
+    def load(start, size):
+        copies = []
+        for p in range(chunks):
+            if remote:
+                c = lax.rem(my_col + p, n_col)
+                src = a_hbm.at[0] if p == 0 else a_full.at[c]
+                lane = pl.multiple_of(c * depth, depth)
+            else:
+                src, lane = a_hbm.at[p], p * depth
+            copies.append(
+                pltpu.make_async_copy(
+                    src.at[pl.ds(start, size), :],
+                    abuf.at[pl.ds(0, size), pl.ds(lane, depth)],
+                    load_sem.at[p],
+                )
+            )
+        for copy in copies:
+            copy.start()
+        for copy in copies:
+            copy.wait()
 
     def square_step(i, unused):
         part = b_ref[pl.ds(pl.multiple_of(i * 32, 32), 32), :].astype(jnp.float32)
@@ -93,8 +196,8 @@
     n_tile = 1024
     n_edges = [(s, min(s + n_tile, cols_pad)) for s in range(0, cols_pad, n_tile)]
 
-    def matmul_tile(start, size, slot):
-        a_tile = abuf.at[slot]
+    def matmul_tile(start, size):
+        a_tile = abuf
         sq = jnp.zeros((size, LANES), jnp.float32)
         for k in range(samples // LANES):
             w = a_tile[0:size, k * LANES:(k + 1) * LANES].astype(jnp.float32)
@@ -123,32 +226,36 @@
         send_r0[1:2, at] = jnp.sum(part.T, 0, keepdims=True)
         return unused
 
-    def tile_step(t, unused):
-        slot = lax.rem(t, 2)
-        start = pl.multiple_of(t * tile, tile)
-        for copy in load(t, start, tile, slot):
-            copy.wait()
-
-        @pl.when(t + 1 < full)
-        def _():
-            for copy in load(t + 1, pl.multiple_of((t + 1) * tile, tile), tile, 1 - slot):
-                copy.start()
-
-        matmul_tile(start, tile, slot)
-        lax.fori_loop(t * (tile // LANES), (t + 1) * (tile // LANES), row_stats, 0)
-        return unused
-
-    if full:
+    def compute(t, start, size):
+        if remote:
+            wait_tile(t, start, size)
+        load(start, size)
+        matmul_tile(start, size)
+        first = t * (tile // LANES)
+        lax.fori_loop(first, first + size // LANES, row_stats, 0)
+
+    if remote:
+
+        def tile_step(t, unused):
+            pass_tile(t, pl.multiple_of(t * tile, tile), tile)
+
+            @pl.when(t > 0)
+            def _():
+                compute(t - 1, pl.multiple_of((t - 1) * tile, tile), tile)
+
+            return unused
+
         lax.fori_loop(0, full, tile_step, 0)
-    if tail:
-        slot = full % 2
-        copies = load(full, full * tile, tail, slot)
-        for copy in copies:
-            copy.start()
-        for copy in copies:
-            copy.wait()
-        matmul_tile(full * tile, tail, slot)
-        lax.fori_loop(full * (tile // LANES), blocks, row_stats, 0)
+        if tail:
+            pass_tile(full, full * tile, tail)
+        compute(full - 1, (full - 1) * tile, tile)
+        if tail:
+            compute(full, full * tile, tail)
+        for copy in b_own + b_passed:
+            copy.wait_send()
+        over_tiles(close_tile)
+    else:
+        over_tiles(compute)
 
     def merge(send, recv, n):
         parts = [send[...]] + [recv[d] for d in range(n - 1)]
@@ -270,28 +377,41 @@
     rows_pad, cols_pad = round_up(rows, LANES), round_up(cols, LANES)
     first = jnp.pad(first_acts, ((0, 0), (0, rows_pad - rows)))
     second = jnp.pad(second_acts, ((0, 0), (0, cols_pad - cols)))
-    b_full = lax.all_gather(second, "row", axis=0, tiled=True)
-    if first.shape[0] % LANES == 0:
-        a_full = lax.all_gather(first.T, "col", axis=0, tiled=False)
+    tile = 512
+    remote = (
+        first.shape[0] % LANES == 0
+        and n_row % 2 == 0
+        and n_col % 2 == 0
+        and rows_pad >= tile
+    )
+    if remote:
+        a_in, b_in = first.T[None], second
+        chunks = n_col
+        gathered = (n_col, rows_pad, first.shape[0])
     else:
-        a_full = lax.all_gather(first, "col", axis=0, tiled=True).T[None]
-    chunks = a_full.shape[0]
-    tile = 512
+        b_in = lax.all_gather(second, "row", axis=0, tiled=True)
+        a_in = lax.all_gather(first, "col", axis=0, tiled=True).T[None]
+        chunks = 1
+        gathered = (1, 16, LANES)
+    tiles = -(-rows_pad // tile)
     rest = ITERS - 1
     f32 = jnp.float32
     vmem = pltpu.VMEM
     dma = pltpu.SemaphoreType.DMA
-    row_out, col_out = pl.pallas_call(
-        functools.partial(kernel, rows, cols, rows * n_row, samples),
+    row_out, col_out, unused = pl.pallas_call(
+        functools.partial(kernel, rows, cols, rows * n_row, samples, tile, remote),
         out_shape=(
             jax.ShapeDtypeStruct((1, rows_pad), f32),
             jax.ShapeDtypeStruct((1, cols_pad), f32),
+            jax.ShapeDtypeStruct(gathered, jnp.bfloat16),
         ),
-        in_specs=[pl.BlockSpec(memory_space=pl.ANY), pl.BlockSpec(memory_space=vmem)],
-        out_specs=(pl.BlockSpec(memory_space=vmem),) * 2,
+        in_specs=[pl.BlockSpec(memory_space=pl.ANY)] * 2,
+        out_specs=(pl.BlockSpec(memory_space=vmem),) * 2
+        + (pl.BlockSpec(memory_space=pl.ANY),),
         scratch_shapes=[
+            vmem((samples, cols_pad), jnp.bfloat16),
             vmem((rows_pad, cols_pad), f32),
-            vmem((2, tile, samples), jnp.bfloat16),
+            vmem((tile, samples), jnp.bfloat16),
             vmem((1, rows_pad), f32),
             vmem((1, cols_pad), f32),
             vmem((1, rows_pad), f32),
@@ -307,7 +427,7 @@
             vmem((n_row - 1, 2, cols_pad), f32),
             vmem((rest, 1, cols_pad), f32),
             vmem((rest, n_row - 1, 1, cols_pad), f32),
-            dma((2, chunks)),
+            dma((chunks,)),
             dma((n_col - 1,)),
             dma((n_col - 1,)),
             dma((rest, n_col - 1)),
@@ -316,11 +436,16 @@
             dma((n_row - 1,)),
             dma((rest, n_row - 1)),
             dma((rest, n_row - 1)),
+            dma,
+            dma((tiles, n_col)),
+            dma((tiles, n_col)),
+            dma((n_row,)),
+            dma((n_row,)),
         ],
         compiler_params=pltpu.CompilerParams(
             collective_id=0, has_side_effects=True, vmem_limit_bytes=67043328
         ),
-    )(a_full, b_full)
+    )(a_in, b_in)
     return row_out[0, :rows], col_out[0, :cols]
 
 

time: 632 us -> 364 us (0.58)
  waiting for transfers between devices: 416 us -> 0 us
  Pallas kernels: 168 us -> 351 us
  local copies, waits for them, and re-layouts: 31 us -> 10.5 us
  between operations: 14.1 us -> 0.65 us
    all_gather x2 -> x0, waiting for transfers between devices: 416 us -> none  [the longest x1 372 us: shards(): a_full = lax.all_gather(first.T, 'col', axis=0, tiled=False)]
    pallas_call x1, Pallas kernels: 168 us -> 351 us  [shards(): pl.pallas_call(functools.partial(kernel, rows, cols, rows * n_row, sample...]
    all_gather x1 -> x0, local copies, waits for them, and re-layouts: 24.9 us -> none  [shards(): a_full = lax.all_gather(first.T, 'col', axis=0, tiled=False)]
  transfers between devices with their start and end apart: 2 -> 0, of which waited for: 2 -> 0; matrix products, arithmetic and copies ran while one was open for 5% -> 0% of each run, Pallas kernels for 0% -> 0%
where the time goes in v2:
time: 364 us
  Pallas kernels  351 us (96%)
  local copies, waits for them, and re-layouts  10.5 us (3%)
    pallas_call x1, Pallas kernels, shards(): pl.pallas_call(functools.partial(kernel, rows, cols, rows * n_row, sample...  351 us
    unnamed x2, local copies, waits for them, and re-layouts  7.52 us

profile of v2, /device:TPU:0, one launch (start us, length us, event | category | flops | bytes accessed | tf_op | source)
XLA Modules:
  0.0 363.6 jit_solution(13341327444729348513)
XLA Ops:
  0.6 4.4 %copy.4 = bf16[256,4736]{0,1:T(8,128)(2,1)} copy(bf16[256,4736]{1,0:T(8,128)(2,1)} %param.2) | data formatting | bytes 4849664 | tf_op args[0]
  5.1 3.1 copy.5
  8.2 1.7 pad.4.b_hbm
  9.8 351.0 %shard_map.41 = (f32[1,4736]{1,0:T(1,128)}, f32[1,2432]{1,0:T(1,128)}, bf16[8,4736,256]{2,1,0:T(8,128)(2,1)}) custom-call(bf16[1,4736,256]{2,1,0:T(8,128)(2,1)} %bitcast.3, bf16[512,2432]{1,0:T(8,128)(2,1)} %pad.4.b_hbm), custom_call_target="tpu_custom_call" | custom-call | tf_op jit(solution)/shard_map/pallas_call | solution.py:401
  360.9 1.4 reduce
  362.2 1.3 slice_reduce_fusion
